TPU v7x, 32 devices: a whole 2x2x4 slice. The times are simulated.
32 devices in a mesh: dp: 2 (over y), expert: 16 (over z, x, core).
Axes of the slice: x: 2, y: 2, z: 4, core: 2. Of those that a mesh axis runs over, the one named last changes fastest.
Arguments:
- routed: bfloat16 [4096, 7168], P(('dp', 'expert')), may hold values from -160 to 160
- expert_ids: int32 [4096, 8], P(('dp', 'expert')), may hold values from 0 to 127, all different within a row
- norm_gain: bfloat16 [7168], replicated, may hold values from 0.099609375 to 1.8984375
- gate_weight: bfloat16 [16, 7168, 2048], P('expert', None, 'dp'), may hold values from -0.0625 to 0.0625
- up_weight: bfloat16 [16, 7168, 2048], P('expert', None, 'dp'), may hold values from -0.0625 to 0.0625
- down_weight: bfloat16 [16, 2048, 7168], P('expert', 'dp'), may hold values from -0.125 to 0.125
- old_place: int32 [16], replicated, may hold values from 0 to 127, as said below
- new_place: int32 [16], replicated, may hold values from 0 to 127, as said below
- probe_ids: int32 [1280], P(('dp', 'expert')), may hold values from 0 to 127
Outputs:
- expert_load: float32 [128], P('expert')
- expert_energy: float32 [128], P('expert')
- probe_out: bfloat16 [1280, 7168], P(('dp', 'expert'))
Inputs may be any that keep to these rules, and one draw needn't show every extreme that they name: `old_place`: 16 different experts. `new_place`: the same 16 experts as old_place, in some order.
All inputs are finite; a program needn't handle non-finite values.
Results may differ from a plain program's by a relative error of at most 0.012.
Values may be sent and summed in bfloat16 or wider, within the bound.
No kernel may reach another device: no remote copies, remote signals or barrier semaphores. Data moves between devices by JAX's collectives and lax.ppermute only.
A program may use at most 128 MiB of HBM per device.

v0:
```python
import math

import jax
import jax.numpy as jnp
from jax import lax
from jax.sharding import PartitionSpec as P

EXP_DEV = 8
TOP = 8


epsilon = 1e-06


def flatten_blocks(array, slots):
    length = array.size // slots
    lanes = math.gcd(length, 128)
    return array.reshape(slots, length // lanes, lanes)


def relay_rows(array, sources):
    shaped = flatten_blocks(array, sources.shape[0])
    moved = lax.all_to_all(
        jnp.take(
            lax.all_to_all(shaped, "expert", split_axis=0, concat_axis=0, tiled=True),
            sources,
            axis=0,
        ),
        "expert",
        split_axis=0,
        concat_axis=0,
        tiled=True,
    )
    return moved.reshape(array.shape)


def expert_block(normed, gate_matrix, up_matrix, down_matrix):
    piece = lax.all_gather(normed, "dp", axis=0, tiled=True)
    gate_value = jnp.dot(piece, gate_matrix, preferred_element_type=jnp.float32)
    up_value = jnp.dot(piece, up_matrix, preferred_element_type=jnp.float32)
    hidden = (jax.nn.silu(gate_value) * up_value).astype(jnp.bfloat16)
    partial_sums = jnp.dot(hidden, down_matrix, preferred_element_type=jnp.float32)
    return lax.psum_scatter(
        partial_sums.astype(jnp.bfloat16), "dp", scatter_dimension=0, tiled=True
    )


def on_device(
    routed,
    expert_ids,
    norm_gain,
    gate_weight,
    up_weight,
    down_weight,
    old_place,
    new_place,
    probe_ids,
):
    slots = lax.axis_size("expert")
    experts = EXP_DEV * slots
    tokens = routed.shape[0] * lax.axis_size("dp") * slots
    features = routed.astype(jnp.float32)
    mean_square = jnp.sum(features * features, axis=1) / routed.shape[1]
    positions = jnp.arange(experts, dtype=jnp.int32)
    onehot = jnp.sum(
        (expert_ids[:, :, None] == positions[None, None, :]).astype(jnp.float32), axis=1
    )
    columns = jnp.stack([jnp.ones_like(mean_square), mean_square])
    local_stats = jnp.dot(columns, onehot, precision=lax.Precision.HIGHEST)
    totals = lax.psum(local_stats, ("dp", "expert"))
    owned = lax.dynamic_slice_in_dim(totals, lax.axis_index("expert") * EXP_DEV, EXP_DEV, 1)
    expert_load = owned[0] * experts / (tokens * TOP)
    expert_energy = owned[1] / owned[0]
    picked_rows = jnp.take(routed, probe_ids, axis=0).astype(jnp.float32)
    scale = lax.rsqrt(jnp.take(mean_square, probe_ids) + epsilon)
    normed = (picked_rows * scale[:, None] * norm_gain.astype(jnp.float32)[None, :]).astype(
        jnp.bfloat16
    )
    slot_index = jnp.arange(slots, dtype=jnp.int32)
    matches = new_place[:, None] == old_place[None, :]
    sources = jnp.sum(jnp.where(matches, slot_index[None, :], 0), axis=1)
    targets = jnp.sum(jnp.where(matches, slot_index[:, None], 0), axis=0)
    arrived = relay_rows(normed, targets)
    computed = expert_block(arrived, gate_weight[0], up_weight[0], down_weight[0])
    probe_out = relay_rows(computed, sources)
    return (expert_load, expert_energy, probe_out)


def solution(mesh):
    in_specs = (
        P(("dp", "expert"), None),
        P(("dp", "expert"), None),
        P(),
        P("expert", None, "dp"),
        P("expert", None, "dp"),
        P("expert", "dp", None),
        P(),
        P(),
        P(("dp", "expert")),
    )
    out_specs = (P("expert"), P("expert"), P(("dp", "expert"), None))
    return jax.shard_map(
        on_device, mesh=mesh, in_specs=in_specs, out_specs=out_specs, check_vma=False
    )
```

profile of v0, /device:TPU:0, one launch (start us, length us, event | category | flops | bytes accessed | tf_op | source)
XLA Modules:
  0.0 210.1 jit_solution(12077049982817701899)
XLA Ops:
  7.2 1.9 multiply_reduce_fusion
  9.2 1.1 mul.44
  10.2 1.6 mul.45
  11.8 1.7 gather_fusion
  13.6 0.8 gather_fusion.1
  14.5 1.8 gather.14
  16.5 1.5 multiply_convert_fusion
  18.0 7.4 %all-to-all-start = ((bf16[16,140,128]{2,1,0:T(8,128)(2,1)}), bf16[16,140,128]{2,1,0:T(8,128)(2,1)S(1)}, u32[]{:S(2)}, u32[]{:S(2)}) async-start(bf16[16,140,128]{2,1,0:T(8,128)(2,1)} %multiply_convert_fusion), calls=%async_computation | async-start | bytes 1179648 | tf_op jit(solution)/shard_map/all_to_all | solution.py:25
  25.7 15.1 %all-to-all-done = bf16[16,140,128]{2,1,0:T(8,128)(2,1)S(1)} async-done(((bf16[16,140,128]{2,1,0:T(8,128)(2,1)}), bf16[16,140,128]{2,1,0:T(8,128)(2,1)S(1)}, u32[]{:S(2)}, u32[]{:S(2)}) %all-to-all-start) | async-done | bytes 573472 | tf_op jit(solution)/shard_map/all_to_all | solution.py:25
  40.8 0.7 gather_fusion.2
  41.6 21.5 %all_to_all.20 = bf16[16,140,128]{2,1,0:T(8,128)(2,1)S(1)} all-to-all(bf16[16,140,128]{2,1,0:T(8,128)(2,1)S(1)} %broadcast_select_fusion.1), channel_id=1, replica_groups=mesh['dp'=2,'expert'=16] {'expert'}, dimensions={0} | all-to-all | bytes 1146880 | tf_op jit(solution)/shard_map/all_to_all | solution.py:23
  63.1 1.4 reshape.51
  64.6 20.8 %all-gather.2.cloned.1.call-done = bf16[80,7168]{1,0:T(8,128)(2,1)} async-done(((bf16[40,7168]{1,0:T(8,128)(2,1)}), bf16[80,7168]{1,0:T(8,128)(2,1)}) %all-gather.2.cloned.1.call-update) | async-done | bytes 1146896 | tf_op jit(solution)/shard_map/all_gather | solution.py:38
  85.4 8.3 %fusion.4 = f32[80,1024]{1,0:T(8,128)S(1)} fusion(bf16[80,7168]{1,0:T(8,128)(2,1)} %all-gather.2.cloned.1.call-done, bf16[1,7168,1024]{2,1,0:T(8,128)(2,1)} %param.14), kind=kOutput, calls=%fused_computation.8 | convolution fusion | flops 1174405120 | bytes 16154624 | tf_op jit(solution)/shard_map/dot_general | solution.py:39
  93.7 15.6 %fusion.6 = bf16[80,7168]{1,0:T(8,128)(2,1)} fusion(bf16[1,1024,7168]{2,1,0:T(8,128)(2,1)} %param.16, bf16[80,7168]{1,0:T(8,128)(2,1)S(1)} %copy-done.1, bf16[1,7168,1024]{2,1,0:T(8,128)(2,1)} %param.15, f32[80,1024]{1,0:T(8,128)S(1)} %fusion.4), kind=kOutput, calls=%fused_computation.10 | convolution fusion | flops 2349875200 | bytes 31981568 | tf_op jit(solution)/shard_map/dot_general | solution.py:42
  109.3 21.6 %reduce-scatter.2.cloned.1.call-done = bf16[40,7168]{1,0:T(8,128)(2,1)} async-done(((bf16[80,7168]{1,0:T(8,128)(2,1)}), bf16[40,7168]{1,0:T(8,128)(2,1)}) %reduce-scatter.2.cloned.1.call-update) | async-done | bytes 573456 | tf_op jit(solution)/shard_map/reduce_scatter | solution.py:43
  130.9 2.6 %reshape.52 = bf16[16,140,128]{2,1,0:T(8,128)(2,1)} reshape(bf16[40,7168]{1,0:T(8,128)(2,1)} %reduce-scatter.2.cloned.1.call-done) | data formatting | bytes 1146880 | tf_op jit(solution)/shard_map/reshape | solution.py:18
  133.6 5.6 %all-to-all-start.2 = ((bf16[16,140,128]{2,1,0:T(8,128)(2,1)}), bf16[16,140,128]{2,1,0:T(8,128)(2,1)S(1)}, u32[]{:S(2)}, u32[]{:S(2)}) async-start(bf16[16,140,128]{2,1,0:T(8,128)(2,1)} %reshape.52), calls=%async_computation.3 | async-start | bytes 1179648 | tf_op jit(solution)/shard_map/all_to_all | solution.py:25
  139.2 15.3 %all-to-all-done.2 = bf16[16,140,128]{2,1,0:T(8,128)(2,1)S(1)} async-done(((bf16[16,140,128]{2,1,0:T(8,128)(2,1)}), bf16[16,140,128]{2,1,0:T(8,128)(2,1)S(1)}, u32[]{:S(2)}, u32[]{:S(2)}) %all-to-all-start.2) | async-done | bytes 573472 | tf_op jit(solution)/shard_map/all_to_all | solution.py:25
  154.6 0.7 gather_fusion.3
  155.2 0.9 broadcast_select_fusion
  156.2 4.5 %all-to-all-start.3 = ((bf16[16,140,128]{2,1,0:T(8,128)(2,1)}), bf16[16,140,128]{2,1,0:T(8,128)(2,1)S(1)}, u32[]{:S(2)}, u32[]{:S(2)}) async-start(bf16[16,140,128]{2,1,0:T(8,128)(2,1)} %broadcast_select_fusion), calls=%async_computation.4 | async-start | bytes 1179648 | tf_op jit(solution)/shard_map/all_to_all | solution.py:23
  161.1 40.1 %psum.7 = f32[2,128]{1,0:T(2,128)S(1)} all-reduce(f32[2,128]{1,0:T(2,128)S(1)} %fusion.25), channel_id=1, replica_groups=mesh['dp'=2,'expert'=16] {'dp','expert'}, use_global_device_ids=true, to_apply=%region_2.0 | all-reduce | flops 256 | bytes 2048 | tf_op jit(solution)/shard_map/psum | solution.py:70
  201.8 1.4 reshape.53
  (40 shorter events, 1.9 us)
Async XLA Ops:
  7.2 2.0 copy-start.2
  9.1 2.7 %copy-start.4 = (s32[40]{0:T(128)S(1)}, s32[40]{0:T(128)}, u32[]{:S(2)}) copy-start(s32[40]{0:T(128)} %param.19) | copy-start | bytes 484
  9.1 2.7 %copy-start = (bf16[128,7168]{1,0:T(8,128)(2,1)S(1)}, bf16[128,7168]{1,0:T(8,128)(2,1)}, u32[]{:S(2)}) copy-start(bf16[128,7168]{1,0:T(8,128)(2,1)} %param.11) | copy-start | bytes 5505028
  16.3 9.1 %copy-start.5 = (s32[16]{0:T(128)S(1)}, s32[16]{0:T(128)}, u32[]{:S(2)}) copy-start(s32[16]{0:T(128)} %param.17) | copy-start | bytes 196
  16.3 9.1 %copy-start.6 = (s32[16]{0:T(128)S(1)}, s32[16]{0:T(128)}, u32[]{:S(2)}) copy-start(s32[16]{0:T(128)} %param.18) | copy-start | bytes 196
  18.0 22.8 %all-to-all-start = ((bf16[16,140,128]{2,1,0:T(8,128)(2,1)}), bf16[16,140,128]{2,1,0:T(8,128)(2,1)S(1)}, u32[]{:S(2)}, u32[]{:S(2)}) async-start(bf16[16,140,128]{2,1,0:T(8,128)(2,1)} %multiply_convert_fusion), calls=%async_computation | async-start | bytes 1179648 | tf_op jit(solution)/shard_map/all_to_all | solution.py:25
  25.4 60.0 %all-gather.2.cloned.1.call-start = ((), (), s32[]{:S(2)}) async-start(), calls=%async_computation.5 | async-start | bytes 1720320 | tf_op jit(solution)/shard_map/all_gather | solution.py:38
  64.5 66.4 %reduce-scatter.2.cloned.1.call-start = ((), (), s32[]{:S(2)}) async-start(), calls=%async_computation.6 | async-start | bytes 1720320 | tf_op jit(solution)/shard_map/reduce_scatter | solution.py:43
  85.4 8.3 %copy-start.1 = (bf16[80,7168]{1,0:T(8,128)(2,1)S(1)}, bf16[80,7168]{1,0:T(8,128)(2,1)}, u32[]{:S(2)}) copy-start(bf16[80,7168]{1,0:T(8,128)(2,1)} %all-gather.2.cloned.1.call-done) | copy-start | bytes 3440644
  133.6 21.0 %all-to-all-start.2 = ((bf16[16,140,128]{2,1,0:T(8,128)(2,1)}), bf16[16,140,128]{2,1,0:T(8,128)(2,1)S(1)}, u32[]{:S(2)}, u32[]{:S(2)}) async-start(bf16[16,140,128]{2,1,0:T(8,128)(2,1)} %reshape.52), calls=%async_computation.3 | async-start | bytes 1179648 | tf_op jit(solution)/shard_map/all_to_all | solution.py:25
  139.2 21.5 %copy-start.3 = (s32[128,8]{0,1:T(8,128)S(1)}, s32[128,8]{0,1:T(8,128)}, u32[]{:S(2)}) copy-start(s32[128,8]{0,1:T(8,128)} %param.12) | copy-start | bytes 12292
  156.2 45.7 %all-to-all-start.3 = ((bf16[16,140,128]{2,1,0:T(8,128)(2,1)}), bf16[16,140,128]{2,1,0:T(8,128)(2,1)S(1)}, u32[]{:S(2)}, u32[]{:S(2)}) async-start(bf16[16,140,128]{2,1,0:T(8,128)(2,1)} %broadcast_select_fusion), calls=%async_computation.4 | async-start | bytes 1179648 | tf_op jit(solution)/shard_map/all_to_all | solution.py:23
Sparse Core Ops, SparseCore 0:
  64.7 20.7 all-gather.1
  109.4 21.4 reduce-scatter.1
where the time goes:
time: 211 us; the launch traced here: 210 us
  waiting for transfers between devices  72.9 us (35%)
  blocking collectives  61.6 us (29%)
  matrix products  24 us (11%)
  starting transfers between devices  17.6 us (8%)
  local copies, waits for them, and re-layouts  14.3 us (7%)
  between operations  14.3 us (7%)
  other arithmetic  5.49 us (3%)
    psum x1, blocking collectives, on_device(): totals = lax.psum(local_stats, ('dp', 'expert'))  40.1 us
    all_to_all x2, waiting for transfers between devices, relay_rows(): lax.all_to_all(shaped, 'expert', split_axis=0, concat_axis=0, tiled=True)  30.4 us
    reduce_scatter x1, waiting for transfers between devices, expert_block(): lax.psum_scatter(partial_sums.astype(jnp.bfloat16), 'dp', scatter_dimensi...  21.6 us
    all_to_all x1, blocking collectives, relay_rows(): lax.all_to_all(jnp.take(lax.all_to_all(shaped, 'expert', split_axis=0, co...  21.5 us
    all_gather x1, waiting for transfers between devices, expert_block(): piece = lax.all_gather(normed, 'dp', axis=0, tiled=True)  20.8 us
    dot_general x1, matrix products, expert_block(): jnp.dot(hidden, down_matrix, preferred_element_type=jnp.float32)  15.6 us
    all_to_all x2, starting transfers between devices, relay_rows(): lax.all_to_all(shaped, 'expert', split_axis=0, concat_axis=0, tiled=True)  13 us
    dot_general x1, matrix products, expert_block(): gate_value = jnp.dot(piece, gate_matrix, preferred_element_type=jnp.float32)  8.25 us
  transfers between devices with their start and end apart: 5, of which 4 were waited for; matrix products, arithmetic and copies ran while one was open for 1% of the time, Pallas kernels for 0%

commit v1 on v0

v1 whole, which is shorter than its diff:
```python
import functools
import math

import jax
import jax.numpy as jnp
from jax import lax
from jax.experimental import pallas as pl
from jax.experimental.pallas import tpu as pltpu
from jax.sharding import PartitionSpec as P

EXP_DEV = 8
TOP = 8
LANES = 128
epsilon = 1e-06
VMEM = pltpu.MemorySpace.VMEM
SMEM = pltpu.MemorySpace.SMEM


def prepare_body(z_ref, probe_ref, routed_ref, ids_ref, gain_ref, stats_ref, *rest):
    pieces, raw_ref = rest[:-1], rest[-1]
    tokens, width = routed_ref.shape
    probes = probe_ref.shape[0]
    experts = stats_ref.shape[1]
    step = 512
    rows = lax.broadcasted_iota(jnp.int32, (probes, tokens), 0)
    lanes = lax.broadcasted_iota(jnp.int32, (probes, tokens), 1)
    wanted = jnp.zeros((probes, tokens), jnp.int32)
    for p in range(probes):
        wanted = jnp.where(rows == p, probe_ref[p], wanted)
    pick = (wanted == lanes).astype(jnp.float32).astype(jnp.bfloat16)

    def gather(k, carry):
        total, chosen = carry
        columns = pl.ds(pl.multiple_of(k * step, step), step)
        block = routed_ref[:, columns]
        values = block.astype(jnp.float32)
        taken = jnp.dot(pick, block, preferred_element_type=jnp.float32)
        raw_ref[:, columns] = taken.astype(jnp.bfloat16)
        for c in range(step // LANES):
            part = values[:, c * LANES : (c + 1) * LANES]
            total = total + part * part
            part = taken[:, c * LANES : (c + 1) * LANES]
            chosen = chosen + part * part
        return total, chosen

    total, chosen = lax.fori_loop(
        0,
        width // step,
        gather,
        (jnp.zeros((tokens, LANES), jnp.float32), jnp.zeros((probes, LANES), jnp.float32)),
    )
    scale = lax.rsqrt(jnp.sum(chosen, axis=1, keepdims=True) / width + epsilon)
    part = width // len(pieces)
    for s, piece in enumerate(pieces):
        start = (z_ref[0] ^ s) * part
        columns = pl.ds(pl.multiple_of(start, LANES), part)
        values = raw_ref[:, columns].astype(jnp.float32)
        gain = gain_ref[:, columns].astype(jnp.float32)
        piece[...] = (values * scale * gain).astype(jnp.bfloat16)
    mean_square = jnp.sum(total.T, axis=0, keepdims=True) / width
    which = lax.broadcasted_iota(jnp.int32, (experts, tokens), 0)
    member = jnp.zeros((experts, tokens), jnp.float32)
    for k in range(ids_ref.shape[0]):
        member = member + (ids_ref[k : k + 1, :] == which).astype(jnp.float32)
    row = lax.broadcasted_iota(jnp.int32, (8, tokens), 0)
    columns = jnp.where(row == 0, 1.0, jnp.broadcast_to(mean_square, (8, tokens)))
    stats_ref[...] = lax.dot_general(
        columns,
        member,
        (((1,), (1,)), ((), ())),
        precision=lax.Precision.HIGHEST,
        preferred_element_type=jnp.float32,
    )


def prepare(z, probe_ids, routed, ids, gain, experts, parts):
    width = routed.shape[1]
    probes = probe_ids.shape[0]
    piece = jax.ShapeDtypeStruct((probes, width // parts), jnp.bfloat16)
    spec = pl.BlockSpec(memory_space=VMEM)
    out = pl.pallas_call(
        prepare_body,
        out_shape=(jax.ShapeDtypeStruct((8, experts), jnp.float32),) + (piece,) * parts,
        in_specs=[pl.BlockSpec(memory_space=SMEM)] * 2 + [spec] * 3,
        out_specs=(spec,) * (parts + 1),
        scratch_shapes=[pltpu.VMEM((probes, width), jnp.bfloat16)],
        cost_estimate=pl.CostEstimate(
            flops=8 * routed.size, bytes_accessed=4 * routed.size, transcendentals=0
        ),
        name="prepare",
    )(z, probe_ids, routed, ids, gain[None])
    return out[0], out[1:]


def gate_up_kernel(groups, *refs):
    xs, refs = refs[:groups], refs[groups:]
    gate_w, up_w, hidden_ref, gate_acc, up_acc = refs
    step = pl.program_id(0)

    @pl.when(step == 0)
    def _():
        gate_acc[...] = jnp.zeros_like(gate_acc)
        up_acc[...] = jnp.zeros_like(up_acc)

    x = jnp.concatenate([x_ref[...] for x_ref in xs], axis=0)
    gate_acc[...] += jnp.dot(x, gate_w[...], preferred_element_type=jnp.float32)
    up_acc[...] += jnp.dot(x, up_w[...], preferred_element_type=jnp.float32)

    @pl.when(step == pl.num_programs(0) - 1)
    def _():
        hidden_ref[...] = (jax.nn.silu(gate_acc[...]) * up_acc[...]).astype(jnp.bfloat16)


def gate_up(xs, gate_w, up_w, block=896):
    rows = sum(x.shape[0] for x in xs)
    width, units = gate_w.shape
    return pl.pallas_call(
        functools.partial(gate_up_kernel, len(xs)),
        grid=(width // block,),
        out_shape=jax.ShapeDtypeStruct((rows, units), jnp.bfloat16),
        in_specs=[pl.BlockSpec((x.shape[0], block), lambda i: (0, i)) for x in xs]
        + [pl.BlockSpec((block, units), lambda i: (i, 0))] * 2,
        out_specs=pl.BlockSpec((rows, units), lambda i: (0, 0)),
        scratch_shapes=[pltpu.VMEM((rows, units), jnp.float32)] * 2,
        cost_estimate=pl.CostEstimate(
            flops=4 * rows * width * units, bytes_accessed=4 * width * units, transcendentals=0
        ),
        name="gate_up",
    )(*xs, gate_w, up_w)


def down_kernel(groups, hidden_ref, down_w, *outs):
    product = jnp.dot(hidden_ref[...], down_w[...], preferred_element_type=jnp.float32)
    rows = product.shape[0] // groups
    for g, out in enumerate(outs):
        out[...] = product[g * rows : (g + 1) * rows].astype(jnp.bfloat16)


def down(hidden, down_w, groups, block=896):
    units, width = down_w.shape
    rows = hidden.shape[0] // groups
    return pl.pallas_call(
        functools.partial(down_kernel, groups),
        grid=(width // block,),
        out_shape=(jax.ShapeDtypeStruct((rows, width), jnp.bfloat16),) * groups,
        in_specs=[
            pl.BlockSpec(hidden.shape, lambda i: (0, 0)),
            pl.BlockSpec((units, block), lambda i: (0, i)),
        ],
        out_specs=(pl.BlockSpec((rows, block), lambda i: (0, i)),) * groups,
        cost_estimate=pl.CostEstimate(
            flops=2 * rows * groups * width * units,
            bytes_accessed=2 * width * units,
            transcendentals=0,
        ),
        name="down",
    )(hidden, down_w)


def swap(value, axis, size, bits):
    return lax.ppermute(value, axis, [(i, i ^ bits) for i in range(size)])


def flatten_blocks(array, slots):
    length = array.size // slots
    lanes = math.gcd(length, 128)
    return array.reshape(slots, length // lanes, lanes)


def relay_rows(array, sources):
    shaped = flatten_blocks(array, sources.shape[0])
    spread = lax.all_to_all(shaped, "expert", split_axis=0, concat_axis=0, tiled=True)
    chosen = jnp.take(spread, sources, axis=0, mode="clip")
    moved = lax.all_to_all(chosen, "expert", split_axis=0, concat_axis=0, tiled=True)
    return moved.reshape(array.shape)


def total_stats(stats, slots, dps):
    bit = 1
    while bit < dps:
        stats = stats + swap(stats, "dp", dps, bit)
        bit *= 2
    bit = 1
    while bit < slots:
        stats = stats + swap(stats, "expert", slots, bit)
        bit *= 2
    return stats


def on_device(
    routed,
    expert_ids,
    norm_gain,
    gate_weight,
    up_weight,
    down_weight,
    old_place,
    new_place,
    probe_ids,
):
    slots = lax.axis_size("expert")
    dps = lax.axis_size("dp")
    experts = EXP_DEV * slots
    tokens = routed.shape[0] * dps * slots
    me = lax.axis_index("expert")
    stats, pieces = prepare(
        jnp.zeros((1,), jnp.int32), probe_ids, routed, expert_ids.T, norm_gain, experts, 1
    )
    slot_index = jnp.arange(slots, dtype=jnp.int32)
    matches = new_place[:, None] == old_place[None, :]
    sources = jnp.sum(jnp.where(matches, slot_index[None, :], 0), axis=1)
    targets = jnp.sum(jnp.where(matches, slot_index[:, None], 0), axis=0)
    arrived = relay_rows(pieces[0], targets)
    rows = [arrived] + [swap(arrived, "dp", dps, s) for s in range(1, dps)]
    hidden = gate_up(rows, gate_weight[0], up_weight[0])
    partial = down(hidden, down_weight[0], dps)
    running = partial[0].astype(jnp.float32)
    for s in range(1, dps):
        running = running + swap(partial[s], "dp", dps, s).astype(jnp.float32)
    probe_out = relay_rows(running.astype(jnp.bfloat16), sources)
    totals = total_stats(stats, slots, dps)
    owned = lax.dynamic_slice_in_dim(totals, me * EXP_DEV, EXP_DEV, 1)
    expert_load = owned[0] * experts / (tokens * TOP)
    expert_energy = owned[1] / owned[0]
    return (expert_load, expert_energy, probe_out)


def solution(mesh):
    in_specs = (
        P(("dp", "expert"), None),
        P(("dp", "expert"), None),
        P(),
        P("expert", None, "dp"),
        P("expert", None, "dp"),
        P("expert", "dp", None),
        P(),
        P(),
        P(("dp", "expert")),
    )
    out_specs = (P("expert"), P("expert"), P(("dp", "expert"), None))
    return jax.shard_map(
        on_device, mesh=mesh, in_specs=in_specs, out_specs=out_specs, check_vma=False
    )
```

time: 211 us -> 157 us (0.74)
  blocking collectives: 61.6 us -> 21.5 us
  Pallas kernels: 0 us -> 28.8 us
  matrix products: 24 us -> 0 us
  between operations: 14.3 us -> 0.73 us
  starting transfers between devices: 17.6 us -> 26.8 us
  waiting for transfers between devices: 72.9 us -> 65.4 us
  local copies, waits for them, and re-layouts: 14.3 us -> 10.6 us
  other arithmetic: 5.49 us -> 1.92 us
    psum x1 -> x0, blocking collectives: 40.1 us -> none  [on_device(): totals = lax.psum(local_stats, ('dp', 'expert'))]
    ppermute x0 -> x7, waiting for transfers between devices: none -> 34.7 us  [swap(): return lax.ppermute(value, axis, [(i, i ^ bits) for i in range(size)])]
    pallas_call x0 -> x3, Pallas kernels: none -> 28.8 us  [the longest x1 14.1 us: gate_up(): pl.pallas_call(functools.partial(gate_up_kernel, len(xs)), grid=(width //...]
    dot_general x3 -> x0, matrix products: 24 us -> none  [the longest x1 15.6 us: expert_block(): jnp.dot(hidden, down_matrix, preferred_element_type=jnp.float32)]
    reduce_scatter x1 -> x0, waiting for transfers between devices: 21.6 us -> none  [expert_block(): lax.psum_scatter(partial_sums.astype(jnp.bfloat16), 'dp', scatter_dimensi...]
    all_gather x1 -> x0, waiting for transfers between devices: 20.8 us -> none  [expert_block(): piece = lax.all_gather(normed, 'dp', axis=0, tiled=True)]
    ppermute x0 -> x7, starting transfers between devices: none -> 11.5 us  [swap(): return lax.ppermute(value, axis, [(i, i ^ bits) for i in range(size)])]
    gather x5 -> x2, local copies, waits for them, and re-layouts: 5.65 us -> 2.1 us  [relay_rows(): chosen = jnp.take(spread, sources, axis=0, mode='clip')]
  transfers between devices with their start and end apart: 5 -> 10, of which waited for: 4 -> 9; matrix products, arithmetic and copies ran while one was open for 1% -> 1% of each run, Pallas kernels for 0% -> 0%
where the time goes in v1:
time: 157 us; the launch traced here: 156 us
  waiting for transfers between devices  65.4 us (42%)
  Pallas kernels  28.8 us (18%)
  starting transfers between devices  26.8 us (17%)
  blocking collectives  21.5 us (14%)
  local copies, waits for them, and re-layouts  10.6 us (7%)
  other arithmetic  1.92 us (1%)
    ppermute x7, waiting for transfers between devices, swap(): return lax.ppermute(value, axis, [(i, i ^ bits) for i in range(size)])  34.7 us
    all_to_all x2, waiting for transfers between devices, relay_rows(): lax.all_to_all(shaped, 'expert', split_axis=0, concat_axis=0, tiled=True)  30.6 us
    all_to_all x1, blocking collectives, relay_rows(): lax.all_to_all(chosen, 'expert', split_axis=0, concat_axis=0, tiled=True)  21.5 us
    pallas_call x1, Pallas kernels, gate_up(): pl.pallas_call(functools.partial(gate_up_kernel, len(xs)), grid=(width //...  14.1 us
    ppermute x7, starting transfers between devices, swap(): return lax.ppermute(value, axis, [(i, i ^ bits) for i in range(size)])  11.5 us
    all_to_all x2, starting transfers between devices, relay_rows(): lax.all_to_all(shaped, 'expert', split_axis=0, concat_axis=0, tiled=True)  11.1 us
    pallas_call x1, Pallas kernels, down(): pl.pallas_call(functools.partial(down_kernel, groups), grid=(width // blo...  9.62 us
    pallas_call x1, Pallas kernels, prepare(): pl.pallas_call(prepare_body, out_shape=(jax.ShapeDtypeStruct((8, experts)...  5.08 us
  transfers between devices with their start and end apart: 10, of which 9 were waited for; matrix products, arithmetic and copies ran while one was open for 1% of the time, Pallas kernels for 0%

profile of v1, /device:TPU:0, one launch (start us, length us, event | category | flops | bytes accessed | tf_op | source)
XLA Modules:
  0.0 155.8 jit_solution(2644242185918345346)
XLA Ops:
  2.0 5.1 %prepare.1 = (f32[8,128]{1,0:T(8,128)}, bf16[40,7168]{1,0:T(8,128)(2,1)}) custom-call(s32[1]{0:T(128)} %constant.6.clone.1.z_ref, s32[40]{0:T(128)} %probe_ref.1, bf16[128,7168]{1,0:T(8,128)(2,1)} %routed_ref.1, s32[8,128]{1,0:T(8,128)} %bitcast.11, bf16[1,7168]{1,0:T(2,128)(2,1)} %broadcast_in_dim.36.gain_ref), custom_call_target="tpu_custom_call" | custom-call | flops 7340032 | bytes 3670016 | tf_op jit(solution)/shard_map/prepare/pallas_call | solution.py:81
  7.0 2.6 %reshape.23 = bf16[16,140,128]{2,1,0:T(8,128)(2,1)} reshape(bf16[40,7168]{1,0:T(8,128)(2,1)} %get-tuple-element.8) | data formatting | bytes 1146880 | tf_op jit(solution)/shard_map/reshape | solution.py:167
  9.7 7.4 %all-to-all-start = ((bf16[16,140,128]{2,1,0:T(8,128)(2,1)}), bf16[16,140,128]{2,1,0:T(8,128)(2,1)S(1)}, u32[]{:S(2)}, u32[]{:S(2)}) async-start(bf16[16,140,128]{2,1,0:T(8,128)(2,1)} %reshape.23), calls=%async_computation | async-start | bytes 1179648 | tf_op jit(solution)/shard_map/all_to_all | solution.py:172
  17.3 15.2 %all-to-all-done = bf16[16,140,128]{2,1,0:T(8,128)(2,1)S(1)} async-done(((bf16[16,140,128]{2,1,0:T(8,128)(2,1)}), bf16[16,140,128]{2,1,0:T(8,128)(2,1)S(1)}, u32[]{:S(2)}, u32[]{:S(2)}) %all-to-all-start) | async-done | bytes 573472 | tf_op jit(solution)/shard_map/all_to_all | solution.py:172
  33.1 21.5 %all_to_all.20 = bf16[16,140,128]{2,1,0:T(8,128)(2,1)S(1)} all-to-all(bf16[16,140,128]{2,1,0:T(8,128)(2,1)S(1)} %gather_fusion), channel_id=1, replica_groups=mesh['dp'=2,'expert'=16] {'expert'}, dimensions={0} | all-to-all | bytes 1146880 | tf_op jit(solution)/shard_map/all_to_all | solution.py:174
  55.3 1.6 %collective-permute-start.5 = (bf16[40,7168]{1,0:T(8,128)(2,1)S(1)}, bf16[40,7168]{1,0:T(8,128)(2,1)S(1)}, u32[]{:S(2)}, u32[]{:S(2)}) collective-permute-start(bf16[40,7168]{1,0:T(8,128)(2,1)S(1)} %reshape.24.refs_0_), channel_id=1, source_target_pairs={{0,16},{16,0},{1,17},{17,1},{2,18},{18,2},{3,19},{19,3},{4,20},{20... | collective-permute-start | bytes 1720328 | tf_op jit(solution)/shard_map/ppermute | solution.py:161
  56.8 13.5 %collective-permute-done.5.refs_1_ = bf16[40,7168]{1,0:T(8,128)(2,1)S(1)} collective-permute-done((bf16[40,7168]{1,0:T(8,128)(2,1)S(1)}, bf16[40,7168]{1,0:T(8,128)(2,1)S(1)}, u32[]{:S(2)}, u32[]{:S(2)}) %collective-permute-start.5) | collective-permute-done | bytes 573472 | tf_op jit(solution)/shard_map/ppermute | solution.py:161
  71.1 14.1 %gate_up.1.hidden_ref = bf16[80,1024]{1,0:T(8,128)(2,1)} custom-call(bf16[40,7168]{1,0:T(8,128)(2,1)} %copy-done, bf16[40,7168]{1,0:T(8,128)(2,1)} %copy-done.1, bf16[7168,1024]{1,0:T(8,128)(2,1)} %bitcast.9, bf16[7168,1024]{1,0:T(8,128)(2,1)} %bitcast.10), custom_call_target="tpu_custom_call" | custom-call | flops 2348810240 | bytes 29360128 | tf_op jit(solution)/shard_map/gate_up/pallas_call | solution.py:117
  85.3 9.6 %down.1 = (bf16[40,7168]{1,0:T(8,128)(2,1)}, bf16[40,7168]{1,0:T(8,128)(2,1)}) custom-call(bf16[80,1024]{1,0:T(8,128)(2,1)} %gate_up.1.hidden_ref, bf16[1024,7168]{1,0:T(8,128)(2,1)} %bitcast.8), custom_call_target="tpu_custom_call" | custom-call | flops 1174405120 | bytes 14680064 | tf_op jit(solution)/shard_map/down/pallas_call | solution.py:142
  94.9 1.5 collective-permute-start.6
  96.4 12.8 %collective-permute-done.6 = bf16[40,7168]{1,0:T(8,128)(2,1)S(1)} collective-permute-done((bf16[40,7168]{1,0:T(8,128)(2,1)}, bf16[40,7168]{1,0:T(8,128)(2,1)S(1)}, u32[]{:S(2)}, u32[]{:S(2)}) %collective-permute-start.6) | collective-permute-done | bytes 573472 | tf_op jit(solution)/shard_map/ppermute | solution.py:161
  110.4 1.6 %reshape.25 = bf16[16,140,128]{2,1,0:T(8,128)(2,1)} reshape(bf16[40,7168]{1,0:T(8,128)(2,1)S(1)} %add_convert_fusion) | data formatting | bytes 1146880 | tf_op jit(solution)/shard_map/reshape | solution.py:167
  112.0 3.7 %all-to-all-start.2 = ((bf16[16,140,128]{2,1,0:T(8,128)(2,1)}), bf16[16,140,128]{2,1,0:T(8,128)(2,1)S(1)}, u32[]{:S(2)}, u32[]{:S(2)}) async-start(bf16[16,140,128]{2,1,0:T(8,128)(2,1)} %reshape.25), calls=%async_computation.2 | async-start | bytes 1179648 | tf_op jit(solution)/shard_map/all_to_all | solution.py:172
  115.8 15.5 %all-to-all-done.2 = bf16[16,140,128]{2,1,0:T(8,128)(2,1)S(1)} async-done(((bf16[16,140,128]{2,1,0:T(8,128)(2,1)}), bf16[16,140,128]{2,1,0:T(8,128)(2,1)S(1)}, u32[]{:S(2)}, u32[]{:S(2)}) %all-to-all-start.2) | async-done | bytes 573472 | tf_op jit(solution)/shard_map/all_to_all | solution.py:172
  132.7 4.3 %all-to-all-start.3 = ((bf16[16,140,128]{2,1,0:T(8,128)(2,1)}), bf16[16,140,128]{2,1,0:T(8,128)(2,1)S(1)}, u32[]{:S(2)}, u32[]{:S(2)}) async-start(bf16[16,140,128]{2,1,0:T(8,128)(2,1)} %gather_fusion.1), calls=%async_computation.3 | async-start | bytes 1179648 | tf_op jit(solution)/shard_map/all_to_all | solution.py:174
  137.0 1.6 %collective-permute-start = (f32[8,128]{1,0:T(8,128)S(1)}, f32[8,128]{1,0:T(8,128)S(1)}, u32[]{:S(2)}, u32[]{:S(2)}) collective-permute-start(f32[8,128]{1,0:T(8,128)S(1)} %copy-done.2), channel_id=1, source_target_pairs={{0,16},{16,0},{1,17},{17,1},{2,18},{18,2},{3,19},{19,3},{4,20},{20... | collective-permute-start | bytes 12296 | tf_op jit(solution)/shard_map/ppermute | solution.py:161
  138.5 2.1 %collective-permute-done = f32[8,128]{1,0:T(8,128)S(1)} collective-permute-done((f32[8,128]{1,0:T(8,128)S(1)}, f32[8,128]{1,0:T(8,128)S(1)}, u32[]{:S(2)}, u32[]{:S(2)}) %collective-permute-start) | collective-permute-done | bytes 4128 | tf_op jit(solution)/shard_map/ppermute | solution.py:161
  141.8 1.9 %collective-permute-start.2 = (f32[8,128]{1,0:T(8,128)S(1)}, f32[8,128]{1,0:T(8,128)S(1)}, u32[]{:S(2)}, u32[]{:S(2)}) collective-permute-start(f32[8,128]{1,0:T(8,128)S(1)} %add.22), channel_id=1, source_target_pairs={{0,2},{1,3},{2,0},{3,1},{4,6},{5,7},{6,4},{7,5},{8,10},{9,11},{10,... | collective-permute-start | bytes 12296 | tf_op jit(solution)/shard_map/ppermute | solution.py:161
  143.7 1.8 %collective-permute-done.2 = f32[8,128]{1,0:T(8,128)S(1)} collective-permute-done((f32[8,128]{1,0:T(8,128)S(1)}, f32[8,128]{1,0:T(8,128)S(1)}, u32[]{:S(2)}, u32[]{:S(2)}) %collective-permute-start.2) | collective-permute-done | bytes 4128 | tf_op jit(solution)/shard_map/ppermute | solution.py:161
  145.5 1.9 %collective-permute-start.3 = (f32[8,128]{1,0:T(8,128)S(1)}, f32[8,128]{1,0:T(8,128)S(1)}, u32[]{:S(2)}, u32[]{:S(2)}) collective-permute-start(f32[8,128]{1,0:T(8,128)S(1)} %add.23), channel_id=1, source_target_pairs={{0,4},{1,5},{2,6},{3,7},{4,0},{5,1},{6,2},{7,3},{8,12},{9,13},{10,... | collective-permute-start | bytes 12296 | tf_op jit(solution)/shard_map/ppermute | solution.py:161
  147.4 1.7 %collective-permute-done.3 = f32[8,128]{1,0:T(8,128)S(1)} collective-permute-done((f32[8,128]{1,0:T(8,128)S(1)}, f32[8,128]{1,0:T(8,128)S(1)}, u32[]{:S(2)}, u32[]{:S(2)}) %collective-permute-start.3) | collective-permute-done | bytes 4128 | tf_op jit(solution)/shard_map/ppermute | solution.py:161
  149.1 3.0 %collective-permute-start.4 = (f32[8,128]{1,0:T(8,128)S(1)}, f32[8,128]{1,0:T(8,128)S(1)}, u32[]{:S(2)}, u32[]{:S(2)}) collective-permute-start(f32[8,128]{1,0:T(8,128)S(1)} %add.24), channel_id=1, source_target_pairs={{0,8},{1,9},{2,10},{3,11},{4,12},{5,13},{6,14},{7,15},{8,0},{9,1},... | collective-permute-start | bytes 12296 | tf_op jit(solution)/shard_map/ppermute | solution.py:161
  152.1 1.7 %collective-permute-done.4 = f32[8,128]{1,0:T(8,128)S(1)} collective-permute-done((f32[8,128]{1,0:T(8,128)S(1)}, f32[8,128]{1,0:T(8,128)S(1)}, u32[]{:S(2)}, u32[]{:S(2)}) %collective-permute-start.4) | collective-permute-done | bytes 4128 | tf_op jit(solution)/shard_map/ppermute | solution.py:161
  154.4 1.4 reshape.26
  (28 shorter events, 8.1 us)
Async XLA Ops:
  2.0 15.1 %copy-start.3 = (s32[16]{0:T(128)S(1)}, s32[16]{0:T(128)}, u32[]{:S(2)}) copy-start(s32[16]{0:T(128)} %param.15) | copy-start | bytes 196
  2.0 15.1 %copy-start.4 = (s32[16]{0:T(128)S(1)}, s32[16]{0:T(128)}, u32[]{:S(2)}) copy-start(s32[16]{0:T(128)} %param.16) | copy-start | bytes 196
  9.7 22.8 %all-to-all-start = ((bf16[16,140,128]{2,1,0:T(8,128)(2,1)}), bf16[16,140,128]{2,1,0:T(8,128)(2,1)S(1)}, u32[]{:S(2)}, u32[]{:S(2)}) async-start(bf16[16,140,128]{2,1,0:T(8,128)(2,1)} %reshape.23), calls=%async_computation | async-start | bytes 1179648 | tf_op jit(solution)/shard_map/all_to_all | solution.py:172
  55.3 15.1 %copy-start = (bf16[40,7168]{1,0:T(8,128)(2,1)}, bf16[40,7168]{1,0:T(8,128)(2,1)S(1)}, u32[]{:S(2)}) copy-start(bf16[40,7168]{1,0:T(8,128)(2,1)S(1)} %reshape.24.refs_0_) | copy-start | bytes 1720324
  55.3 15.1 %collective-permute-start.5 = (bf16[40,7168]{1,0:T(8,128)(2,1)S(1)}, bf16[40,7168]{1,0:T(8,128)(2,1)S(1)}, u32[]{:S(2)}, u32[]{:S(2)}) collective-permute-start(bf16[40,7168]{1,0:T(8,128)(2,1)S(1)} %reshape.24.refs_0_), channel_id=1, source_target_pairs={{0,16},{16,0},{1,17},{17,1},{2,18},{18,2},{3,19},{19,3},{4,20},{20... | collective-permute-start | bytes 1720328 | tf_op jit(solution)/shard_map/ppermute | solution.py:161
  70.3 0.8 copy-start.1
  94.9 14.4 %collective-permute-start.6 = (bf16[40,7168]{1,0:T(8,128)(2,1)}, bf16[40,7168]{1,0:T(8,128)(2,1)S(1)}, u32[]{:S(2)}, u32[]{:S(2)}) collective-permute-start(bf16[40,7168]{1,0:T(8,128)(2,1)} %get-tuple-element.10), channel_id=1, source_target_pairs={{0,16},{16,0},{1,17},{17,1},{2,18},{18,2},{3,19},{19,3},{4,20},{20... | collective-permute-start | bytes 1720328 | tf_op jit(solution)/shard_map/ppermute | solution.py:161
  112.0 24.9 %copy-start.2 = (f32[8,128]{1,0:T(8,128)S(1)}, f32[8,128]{1,0:T(8,128)}, u32[]{:S(2)}) copy-start(f32[8,128]{1,0:T(8,128)} %get-tuple-element.7) | copy-start | bytes 12292
  112.0 19.2 %all-to-all-start.2 = ((bf16[16,140,128]{2,1,0:T(8,128)(2,1)}), bf16[16,140,128]{2,1,0:T(8,128)(2,1)S(1)}, u32[]{:S(2)}, u32[]{:S(2)}) async-start(bf16[16,140,128]{2,1,0:T(8,128)(2,1)} %reshape.25), calls=%async_computation.2 | async-start | bytes 1179648 | tf_op jit(solution)/shard_map/all_to_all | solution.py:172
  132.7 21.7 %all-to-all-start.3 = ((bf16[16,140,128]{2,1,0:T(8,128)(2,1)}), bf16[16,140,128]{2,1,0:T(8,128)(2,1)S(1)}, u32[]{:S(2)}, u32[]{:S(2)}) async-start(bf16[16,140,128]{2,1,0:T(8,128)(2,1)} %gather_fusion.1), calls=%async_computation.3 | async-start | bytes 1179648 | tf_op jit(solution)/shard_map/all_to_all | solution.py:174
  137.0 3.7 %collective-permute-start = (f32[8,128]{1,0:T(8,128)S(1)}, f32[8,128]{1,0:T(8,128)S(1)}, u32[]{:S(2)}, u32[]{:S(2)}) collective-permute-start(f32[8,128]{1,0:T(8,128)S(1)} %copy-done.2), channel_id=1, source_target_pairs={{0,16},{16,0},{1,17},{17,1},{2,18},{18,2},{3,19},{19,3},{4,20},{20... | collective-permute-start | bytes 12296 | tf_op jit(solution)/shard_map/ppermute | solution.py:161
  140.6 1.2 collective-permute-start.1
  141.8 3.7 %collective-permute-start.2 = (f32[8,128]{1,0:T(8,128)S(1)}, f32[8,128]{1,0:T(8,128)S(1)}, u32[]{:S(2)}, u32[]{:S(2)}) collective-permute-start(f32[8,128]{1,0:T(8,128)S(1)} %add.22), channel_id=1, source_target_pairs={{0,2},{1,3},{2,0},{3,1},{4,6},{5,7},{6,4},{7,5},{8,10},{9,11},{10,... | collective-permute-start | bytes 12296 | tf_op jit(solution)/shard_map/ppermute | solution.py:161
  145.5 3.6 %collective-permute-start.3 = (f32[8,128]{1,0:T(8,128)S(1)}, f32[8,128]{1,0:T(8,128)S(1)}, u32[]{:S(2)}, u32[]{:S(2)}) collective-permute-start(f32[8,128]{1,0:T(8,128)S(1)} %add.23), channel_id=1, source_target_pairs={{0,4},{1,5},{2,6},{3,7},{4,0},{5,1},{6,2},{7,3},{8,12},{9,13},{10,... | collective-permute-start | bytes 12296 | tf_op jit(solution)/shard_map/ppermute | solution.py:161
  149.1 4.7 %collective-permute-start.4 = (f32[8,128]{1,0:T(8,128)S(1)}, f32[8,128]{1,0:T(8,128)S(1)}, u32[]{:S(2)}, u32[]{:S(2)}) collective-permute-start(f32[8,128]{1,0:T(8,128)S(1)} %add.24), channel_id=1, source_target_pairs={{0,8},{1,9},{2,10},{3,11},{4,12},{5,13},{6,14},{7,15},{8,0},{9,1},... | collective-permute-start | bytes 12296 | tf_op jit(solution)/shard_map/ppermute | solution.py:161
